TPU v7x, 32 devices: a whole 2x2x4 slice. The times are simulated.
32 devices in a mesh: row: 8 (over y, x, core), col: 4 (over z).
Axes of the slice: x: 2, y: 2, z: 4, core: 2. Of those that a mesh axis runs over, the one named last changes fastest.
Arguments:
- features: bfloat16 [16384, 256], P(('row', 'col')), may hold values from -1 to 3
- in_degree: int32 [16384], P(('row', 'col')), may hold values from 512 to 2047
- tile_index: int32 [8192, 2], P(('row', 'col')), may hold values from 0 to 31, as said below
- tile_count: int32 [32], P(('row', 'col')), may hold values from 1 to 256, as said below
- adjacency_tiles: bfloat16 [8192, 128, 128], P(('row', 'col')), may hold values from 0 to 1, as said below
- projection: bfloat16 [512, 256], replicated, may hold values from -0.25 to 0.25
- out_bias: float32 [256], replicated, may hold values from -3 to 3
Outputs:
- hidden_out: bfloat16 [16384, 256], P(('row', 'col'))
Inputs may be any that keep to these rules, and one draw needn't show every extreme that they name: `tile_index`: column 0 is a local row block below 16, column 1 a local column block below 32, in every slot. `tile_count`: slots at or beyond the count hold tiles and indices that must be ignored; some device has all 256 slots live in every draw. `adjacency_tiles`: entries are 0 or 1.
All inputs are finite; a program needn't handle non-finite values.
Results may differ from a plain program's by a relative error of at most 0.0034.
Values may be sent and summed in bfloat16 or wider, within the bound.
A program may use at most 128 MiB of HBM per device.

v0:
```python
import jax
import jax.numpy as jnp
from jax import lax
from jax.sharding import PartitionSpec as P

BLK = 32


def block_terms(running, col_blocks, index_block, tile_block, live_block):
    picked = col_blocks[index_block[:, 1]]
    kept = jnp.where(live_block[:, None, None], tile_block, jnp.zeros_like(tile_block))
    product = jnp.einsum("kij,kjf->kif", kept, picked, preferred_element_type=jnp.float32)
    flattened = product.reshape(product.shape[0], -1)
    return running.at[index_block[:, 0]].add(flattened)


def local(features, in_degree, tile_index, tile_count, adjacency_tiles, projection, out_bias):
    feat_width = features.shape[1]
    tile_size = adjacency_tiles.shape[1]
    slot_total = adjacency_tiles.shape[0]
    gathered = lax.all_gather(features, "row", axis=0, tiled=True)
    col_blocks = gathered.reshape(gathered.shape[0] // tile_size, tile_size, feat_width)
    row_blocks = features.shape[0] * lax.axis_size("col") // tile_size
    live_count = tile_count[0]
    zeroed = jnp.zeros((row_blocks, tile_size * feat_width), jnp.float32)

    def one_step(running, offset):
        index_block = lax.dynamic_slice_in_dim(tile_index, offset, BLK, 0)
        tile_block = lax.dynamic_slice_in_dim(adjacency_tiles, offset, BLK, 0)
        live_block = offset + jnp.arange(BLK, dtype=jnp.int32) < live_count
        return (block_terms(running, col_blocks, index_block, tile_block, live_block), None)

    summed, _ = lax.scan(one_step, zeroed, jnp.arange(0, slot_total, BLK, dtype=jnp.int32))
    partial_value = summed.reshape(row_blocks * tile_size, feat_width)
    own_sums = lax.psum_scatter(partial_value, "col", scatter_dimension=0, tiled=True)
    neighbour_mean = (own_sums / in_degree[:, None].astype(jnp.float32)).astype(jnp.bfloat16)
    joined = jnp.concatenate([features, neighbour_mean], axis=1)
    mixed = jnp.dot(joined, projection, preferred_element_type=jnp.float32) + out_bias[None, :]
    return jnp.maximum(mixed, 0.0).astype(jnp.bfloat16)


def solution(mesh):
    return jax.shard_map(
        local,
        mesh=mesh,
        in_specs=(
            P(("row", "col"), None),
            P(("row", "col")),
            P(("row", "col"), None),
            P(("row", "col")),
            P(("row", "col"), None, None),
            P(),
            P(),
        ),
        out_specs=P(("row", "col"), None),
        check_vma=False,
    )
```

profile of v0, /device:TPU:0, one launch (start us, length us, event | category | flops | bytes accessed | tf_op | source)
XLA Modules:
  0.0 272.5 jit_solution(9755557317256504715)
XLA Ops:
  6.5 0.7 all-gather.2.cloned.1.call-update
  7.3 32.4 %all-gather.2.cloned.1.call-done = bf16[4096,256]{1,0:T(8,128)(2,1)} async-done(((bf16[512,256]{1,0:T(8,128)(2,1)}), bf16[4096,256]{1,0:T(8,128)(2,1)}) %all-gather.2.cloned.1.call-update) | async-done | bytes 2097168 | tf_op jit(solution)/shard_map/all_gather | solution.py:21
  39.8 0.1 broadcast_in_dim.13
  39.9 178.2 %while.10 = (s32[]{:T(128)}, f32[16,32768]{1,0:T(8,128)S(1)}, s32[8]{0:T(128)S(1)}, s32[256,2]{0,1:T(2,128)S(1)}, s32[]{:T(128)}, /*index=5*/bf16[256,128,128]{2...) while((s32[]{:T(128)}, f32[16,32768]{1,0:T(8,128)S(1)}, s32[8]{0:T(128)S(1)}, ...), condition=%wide.region_2.3_spmd, body=%wide.region_0.2_spmd.sunk | while | flops 270009600 | bytes 32511596 | solution.py:33
  39.9 0.7 dynamic_slice.20
  42.6 0.1 constant_dynamic-slice_fusion.2
  42.7 3.6 %gather_fusion = bf16[32,128,256]{2,1,0:T(8,128)(2,1)} fusion(bf16[32,128,256]{2,1,0:T(8,128)(2,1)} %get-tuple-element.132, s32[1024]{0:T(1024)S(1)} %pad_clamp_fusion.2), kind=kCustom, calls=%fused_computation.clone.1 | custom fusion | bytes 4194432 | tf_op jit(solution)/shard_map/while/body/eval_jaxpr/gather | solution.py:10
  46.3 1.3 add_compare_fusion.2
  47.7 2.7 fusion.24
  50.4 4.4 %copy.10 = f32[4,8,128,256]{3,1,2,0:T(8,128)} copy(f32[4,8,128,256]{3,2,1,0:T(8,128)S(1)} %bitcast.21) | data formatting | bytes 8388608 | tf_op jit(solution)/shard_map/while
  54.7 7.4 %scatter_fusion = f32[16,32768]{1,0:T(8,128)S(1)} fusion(f32[16,32768]{1,0:T(8,128)S(1)} %get-tuple-element.117, s32[32]{0:T(128)S(1)} %get-tuple-element.104, f32[32,32768]{1,0:T(8,128)} %bitcast.22), kind=kCustom, calls=%fused_computation.1.clone.1 | custom fusion | flops 1048576 | bytes 12583040 | tf_op jit(solution)/shard_map/while/body/eval_jaxpr/scatter-add | solution.py:14
  62.2 0.7 dynamic_slice.20
  64.9 0.1 constant_dynamic-slice_fusion.2
  65.0 3.6 %gather_fusion = bf16[32,128,256]{2,1,0:T(8,128)(2,1)} fusion(bf16[32,128,256]{2,1,0:T(8,128)(2,1)} %get-tuple-element.132, s32[1024]{0:T(1024)S(1)} %pad_clamp_fusion.2), kind=kCustom, calls=%fused_computation.clone.1 | custom fusion | bytes 4194432 | tf_op jit(solution)/shard_map/while/body/eval_jaxpr/gather | solution.py:10
  68.6 1.3 add_compare_fusion.2
  69.9 2.7 fusion.24
  72.6 4.4 %copy.10 = f32[4,8,128,256]{3,1,2,0:T(8,128)} copy(f32[4,8,128,256]{3,2,1,0:T(8,128)S(1)} %bitcast.21) | data formatting | bytes 8388608 | tf_op jit(solution)/shard_map/while
  77.0 7.4 %scatter_fusion = f32[16,32768]{1,0:T(8,128)S(1)} fusion(f32[16,32768]{1,0:T(8,128)S(1)} %get-tuple-element.117, s32[32]{0:T(128)S(1)} %get-tuple-element.104, f32[32,32768]{1,0:T(8,128)} %bitcast.22), kind=kCustom, calls=%fused_computation.1.clone.1 | custom fusion | flops 1048576 | bytes 12583040 | tf_op jit(solution)/shard_map/while/body/eval_jaxpr/scatter-add | solution.py:14
  84.5 0.7 dynamic_slice.20
  87.2 0.1 constant_dynamic-slice_fusion.2
  87.3 3.6 %gather_fusion = bf16[32,128,256]{2,1,0:T(8,128)(2,1)} fusion(bf16[32,128,256]{2,1,0:T(8,128)(2,1)} %get-tuple-element.132, s32[1024]{0:T(1024)S(1)} %pad_clamp_fusion.2), kind=kCustom, calls=%fused_computation.clone.1 | custom fusion | bytes 4194432 | tf_op jit(solution)/shard_map/while/body/eval_jaxpr/gather | solution.py:10
  90.9 1.3 add_compare_fusion.2
  92.2 2.7 fusion.24
  94.9 4.4 %copy.10 = f32[4,8,128,256]{3,1,2,0:T(8,128)} copy(f32[4,8,128,256]{3,2,1,0:T(8,128)S(1)} %bitcast.21) | data formatting | bytes 8388608 | tf_op jit(solution)/shard_map/while
  99.3 7.4 %scatter_fusion = f32[16,32768]{1,0:T(8,128)S(1)} fusion(f32[16,32768]{1,0:T(8,128)S(1)} %get-tuple-element.117, s32[32]{0:T(128)S(1)} %get-tuple-element.104, f32[32,32768]{1,0:T(8,128)} %bitcast.22), kind=kCustom, calls=%fused_computation.1.clone.1 | custom fusion | flops 1048576 | bytes 12583040 | tf_op jit(solution)/shard_map/while/body/eval_jaxpr/scatter-add | solution.py:14
  106.7 0.7 dynamic_slice.20
  109.4 0.1 constant_dynamic-slice_fusion.2
  109.5 3.6 %gather_fusion = bf16[32,128,256]{2,1,0:T(8,128)(2,1)} fusion(bf16[32,128,256]{2,1,0:T(8,128)(2,1)} %get-tuple-element.132, s32[1024]{0:T(1024)S(1)} %pad_clamp_fusion.2), kind=kCustom, calls=%fused_computation.clone.1 | custom fusion | bytes 4194432 | tf_op jit(solution)/shard_map/while/body/eval_jaxpr/gather | solution.py:10
  113.1 1.3 add_compare_fusion.2
  114.5 2.7 fusion.24
  117.2 4.4 %copy.10 = f32[4,8,128,256]{3,1,2,0:T(8,128)} copy(f32[4,8,128,256]{3,2,1,0:T(8,128)S(1)} %bitcast.21) | data formatting | bytes 8388608 | tf_op jit(solution)/shard_map/while
  121.5 7.4 %scatter_fusion = f32[16,32768]{1,0:T(8,128)S(1)} fusion(f32[16,32768]{1,0:T(8,128)S(1)} %get-tuple-element.117, s32[32]{0:T(128)S(1)} %get-tuple-element.104, f32[32,32768]{1,0:T(8,128)} %bitcast.22), kind=kCustom, calls=%fused_computation.1.clone.1 | custom fusion | flops 1048576 | bytes 12583040 | tf_op jit(solution)/shard_map/while/body/eval_jaxpr/scatter-add | solution.py:14
  129.0 0.7 dynamic_slice.20
  131.7 0.1 constant_dynamic-slice_fusion.2
  131.8 3.6 %gather_fusion = bf16[32,128,256]{2,1,0:T(8,128)(2,1)} fusion(bf16[32,128,256]{2,1,0:T(8,128)(2,1)} %get-tuple-element.132, s32[1024]{0:T(1024)S(1)} %pad_clamp_fusion.2), kind=kCustom, calls=%fused_computation.clone.1 | custom fusion | bytes 4194432 | tf_op jit(solution)/shard_map/while/body/eval_jaxpr/gather | solution.py:10
  135.4 1.3 add_compare_fusion.2
  136.7 2.7 fusion.24
  139.4 4.4 %copy.10 = f32[4,8,128,256]{3,1,2,0:T(8,128)} copy(f32[4,8,128,256]{3,2,1,0:T(8,128)S(1)} %bitcast.21) | data formatting | bytes 8388608 | tf_op jit(solution)/shard_map/while
  143.8 7.4 %scatter_fusion = f32[16,32768]{1,0:T(8,128)S(1)} fusion(f32[16,32768]{1,0:T(8,128)S(1)} %get-tuple-element.117, s32[32]{0:T(128)S(1)} %get-tuple-element.104, f32[32,32768]{1,0:T(8,128)} %bitcast.22), kind=kCustom, calls=%fused_computation.1.clone.1 | custom fusion | flops 1048576 | bytes 12583040 | tf_op jit(solution)/shard_map/while/body/eval_jaxpr/scatter-add | solution.py:14
  151.3 0.7 dynamic_slice.20
  154.0 0.1 constant_dynamic-slice_fusion.2
  154.1 3.6 %gather_fusion = bf16[32,128,256]{2,1,0:T(8,128)(2,1)} fusion(bf16[32,128,256]{2,1,0:T(8,128)(2,1)} %get-tuple-element.132, s32[1024]{0:T(1024)S(1)} %pad_clamp_fusion.2), kind=kCustom, calls=%fused_computation.clone.1 | custom fusion | bytes 4194432 | tf_op jit(solution)/shard_map/while/body/eval_jaxpr/gather | solution.py:10
  157.7 1.3 add_compare_fusion.2
  159.0 2.7 fusion.24
  161.7 4.4 %copy.10 = f32[4,8,128,256]{3,1,2,0:T(8,128)} copy(f32[4,8,128,256]{3,2,1,0:T(8,128)S(1)} %bitcast.21) | data formatting | bytes 8388608 | tf_op jit(solution)/shard_map/while
  166.1 7.4 %scatter_fusion = f32[16,32768]{1,0:T(8,128)S(1)} fusion(f32[16,32768]{1,0:T(8,128)S(1)} %get-tuple-element.117, s32[32]{0:T(128)S(1)} %get-tuple-element.104, f32[32,32768]{1,0:T(8,128)} %bitcast.22), kind=kCustom, calls=%fused_computation.1.clone.1 | custom fusion | flops 1048576 | bytes 12583040 | tf_op jit(solution)/shard_map/while/body/eval_jaxpr/scatter-add | solution.py:14
  173.5 0.7 dynamic_slice.20
  176.2 0.1 constant_dynamic-slice_fusion.2
  176.3 3.6 %gather_fusion = bf16[32,128,256]{2,1,0:T(8,128)(2,1)} fusion(bf16[32,128,256]{2,1,0:T(8,128)(2,1)} %get-tuple-element.132, s32[1024]{0:T(1024)S(1)} %pad_clamp_fusion.2), kind=kCustom, calls=%fused_computation.clone.1 | custom fusion | bytes 4194432 | tf_op jit(solution)/shard_map/while/body/eval_jaxpr/gather | solution.py:10
  180.0 1.3 add_compare_fusion.2
  181.3 2.7 fusion.24
  184.0 4.4 %copy.10 = f32[4,8,128,256]{3,1,2,0:T(8,128)} copy(f32[4,8,128,256]{3,2,1,0:T(8,128)S(1)} %bitcast.21) | data formatting | bytes 8388608 | tf_op jit(solution)/shard_map/while
  188.3 7.4 %scatter_fusion = f32[16,32768]{1,0:T(8,128)S(1)} fusion(f32[16,32768]{1,0:T(8,128)S(1)} %get-tuple-element.117, s32[32]{0:T(128)S(1)} %get-tuple-element.104, f32[32,32768]{1,0:T(8,128)} %bitcast.22), kind=kCustom, calls=%fused_computation.1.clone.1 | custom fusion | flops 1048576 | bytes 12583040 | tf_op jit(solution)/shard_map/while/body/eval_jaxpr/scatter-add | solution.py:14
  195.8 0.7 dynamic_slice.20
  198.6 3.6 %gather_fusion = bf16[32,128,256]{2,1,0:T(8,128)(2,1)} fusion(bf16[32,128,256]{2,1,0:T(8,128)(2,1)} %get-tuple-element.132, s32[1024]{0:T(1024)S(1)} %pad_clamp_fusion.2), kind=kCustom, calls=%fused_computation.clone.1 | custom fusion | bytes 4194432 | tf_op jit(solution)/shard_map/while/body/eval_jaxpr/gather | solution.py:10
  202.2 1.3 add_compare_fusion.2
  203.6 2.7 fusion.24
  206.2 4.4 %copy.10 = f32[4,8,128,256]{3,1,2,0:T(8,128)} copy(f32[4,8,128,256]{3,2,1,0:T(8,128)S(1)} %bitcast.21) | data formatting | bytes 8388608 | tf_op jit(solution)/shard_map/while
  210.6 7.4 %scatter_fusion = f32[16,32768]{1,0:T(8,128)S(1)} fusion(f32[16,32768]{1,0:T(8,128)S(1)} %get-tuple-element.117, s32[32]{0:T(128)S(1)} %get-tuple-element.104, f32[32,32768]{1,0:T(8,128)} %bitcast.22), kind=kCustom, calls=%fused_computation.1.clone.1 | custom fusion | flops 1048576 | bytes 12583040 | tf_op jit(solution)/shard_map/while/body/eval_jaxpr/scatter-add | solution.py:14
  218.1 1.5 reshape.18
  219.6 0.7 copy-done.3
  220.3 43.1 %reduce-scatter.2.cloned.1.call-done = f32[512,256]{1,0:T(8,128)} async-done(((f32[2048,256]{1,0:T(8,128)}), f32[512,256]{1,0:T(8,128)}) %reduce-scatter.2.cloned.1.call-update) | async-done | bytes 524304 | tf_op jit(solution)/shard_map/reduce_scatter | solution.py:35
  263.4 1.2 divide_convert_fusion
  264.6 1.0 fusion.10
  (31 shorter events, 0.3 us)
Async XLA Ops:
  6.5 258.1 %copy-start = (bf16[512,256]{1,0:T(8,128)(2,1)S(1)}, bf16[512,256]{1,0:T(8,128)(2,1)}, u32[]{:S(2)}) copy-start(bf16[512,256]{1,0:T(8,128)(2,1)} %param.14) | copy-start | bytes 786436
  6.5 33.4 %copy-start.2 = (s32[256,2]{0,1:T(2,128)S(1)}, s32[256,2]{0,1:T(2,128)}, u32[]{:S(2)}) copy-start(s32[256,2]{0,1:T(2,128)} %param.11) | copy-start | bytes 6148
  6.5 33.2 %all-gather.2.cloned.1.call-start = ((), (), s32[]{:S(2)}) async-start(), calls=%async_computation.1 | async-start | bytes 2359296 | tf_op jit(solution)/shard_map/all_gather | solution.py:21
  7.3 256.2 %reduce-scatter.2.cloned.1.call-start = ((), (), s32[]{:S(2)}) async-start(), calls=%async_computation.2 | async-start | bytes 2621440 | tf_op jit(solution)/shard_map/reduce_scatter | solution.py:35
  219.6 0.7 copy-start.3
  219.6 45.0 %copy-start.1 = (bf16[512,256]{1,0:T(8,128)(2,1)S(1)}, bf16[512,256]{1,0:T(8,128)(2,1)}, u32[]{:S(2)}) copy-start(bf16[512,256]{1,0:T(8,128)(2,1)} %param.9) | copy-start | bytes 786436
  219.6 45.0 %copy-start.4 = (f32[256]{0:T(256)S(1)}, f32[256]{0:T(256)}, u32[]{:S(2)}) copy-start(f32[256]{0:T(256)} %param.15) | copy-start | bytes 3076
Sparse Core Ops, SparseCore 0:
  9.2 30.4 all-gather.1
  219.8 43.6 reduce-scatter.1
where the time goes:
time: 274 us; the launch traced here: 273 us
  waiting for transfers between devices  76.3 us (28%)
  local copies, waits for them, and re-layouts  72.1 us (26%)
  other arithmetic  71.5 us (26%)
  matrix products  22.5 us (8%)
  loops' own time  16.7 us (6%)
  between operations  13.5 us (5%)
    scatter-add x8, other arithmetic, block_terms(): return running.at[index_block[:, 0]].add(flattened)  59.6 us
    reduce_scatter x1, waiting for transfers between devices, local(): lax.psum_scatter(partial_value, 'col', scatter_dimension=0, tiled=True)  43.1 us
    while x8, local copies, waits for them, and re-layouts  35 us
    all_gather x1, waiting for transfers between devices, local(): gathered = lax.all_gather(features, 'row', axis=0, tiled=True)  32.4 us
    gather x8, local copies, waits for them, and re-layouts, block_terms(): picked = col_blocks[index_block[:, 1]]  28.9 us
    dot_general x8, matrix products, block_terms(): jnp.einsum('kij,kjf->kif', kept, picked, preferred_element_type=jnp.float32)  21.4 us
    another operation x1, loops' own time, local(): lax.scan(one_step, zeroed, jnp.arange(0, slot_total, BLK, dtype=jnp.int32))  16.7 us
    lt x8, other arithmetic, one_step(): live_block = offset + jnp.arange(BLK, dtype=jnp.int32) < live_count  10.6 us
  transfers between devices with their start and end apart: 2, of which 2 were waited for; matrix products, arithmetic and copies ran while one was open for 0% of the time, Pallas kernels for 0%

commit v1 on v0

--- a/solution.py
+++ b/solution.py
@@ -18,7 +18,12 @@
     feat_width = features.shape[1]
     tile_size = adjacency_tiles.shape[1]
     slot_total = adjacency_tiles.shape[0]
-    gathered = lax.all_gather(features, "row", axis=0, tiled=True)
+    ring = [features]
+    for hop in range(7):
+        ring.append(lax.ppermute(ring[-1], "row", [(dev, (dev + 1) % 8) for dev in range(8)]))
+    gathered = jnp.roll(
+        jnp.concatenate(ring[::-1], axis=0), (lax.axis_index("row") + 1) * ring[0].shape[0], axis=0
+    )
     col_blocks = gathered.reshape(gathered.shape[0] // tile_size, tile_size, feat_width)
     row_blocks = features.shape[0] * lax.axis_size("col") // tile_size
     live_count = tile_count[0]

time: 274 us -> 292 us (1.066)
  waiting for transfers between devices: 76.3 us -> 92.1 us
    ppermute x0 -> x7, waiting for transfers between devices: none -> 47.3 us  [local(): lax.ppermute(ring[-1], 'row', [(dev, (dev + 1) % 8) for dev in range(8)])]
    all_gather x1 -> x0, waiting for transfers between devices: 32.4 us -> none  [local(): gathered = lax.all_gather(features, 'row', axis=0, tiled=True)]
  transfers between devices with their start and end apart: 2 -> 8, of which waited for: 2 -> 8; matrix products, arithmetic and copies ran while one was open for 0% -> 0% of each run, Pallas kernels for 0% -> 0%
where the time goes in v1:
time: 292 us; the launch traced here: 291 us
  waiting for transfers between devices  92.1 us (32%)
  local copies, waits for them, and re-layouts  74.1 us (25%)
  other arithmetic  71.5 us (24%)
  matrix products  22.5 us (8%)
  loops' own time  16.6 us (6%)
  between operations  13.6 us (5%)
    scatter-add x8, other arithmetic, block_terms(): return running.at[index_block[:, 0]].add(flattened)  59.6 us
    ppermute x7, waiting for transfers between devices, local(): lax.ppermute(ring[-1], 'row', [(dev, (dev + 1) % 8) for dev in range(8)])  47.3 us
    reduce_scatter x1, waiting for transfers between devices, local(): lax.psum_scatter(partial_value, 'col', scatter_dimension=0, tiled=True)  44.8 us
    while x8, local copies, waits for them, and re-layouts  35.1 us
    gather x8, local copies, waits for them, and re-layouts, block_terms(): picked = col_blocks[index_block[:, 1]]  28.8 us
    dot_general x8, matrix products, block_terms(): jnp.einsum('kij,kjf->kif', kept, picked, preferred_element_type=jnp.float32)  21.4 us
    another operation x1, loops' own time, local(): lax.scan(one_step, zeroed, jnp.arange(0, slot_total, BLK, dtype=jnp.int32))  16.6 us
    lt x8, other arithmetic, one_step(): live_block = offset + jnp.arange(BLK, dtype=jnp.int32) < live_count  10.6 us
  transfers between devices with their start and end apart: 8, of which 8 were waited for; matrix products, arithmetic and copies ran while one was open for 0% of the time, Pallas kernels for 0%

profile of v1, /device:TPU:0, one launch (start us, length us, event | category | flops | bytes accessed | tf_op | source)
XLA Modules:
  0.0 290.9 jit_solution(3398965830454677907)
XLA Ops:
  6.5 0.5 collective-permute-start
  7.0 7.2 %collective-permute-done = bf16[512,256]{1,0:T(8,128)(2,1)S(1)} collective-permute-done((bf16[512,256]{1,0:T(8,128)(2,1)}, bf16[512,256]{1,0:T(8,128)(2,1)S(1)}, u32[]{:S(2)}, u32[]{:S(2)}) %collective-permute-start) | collective-permute-done | bytes 262176 | tf_op jit(solution)/shard_map/ppermute | solution.py:23
  14.2 6.7 %collective-permute-done.1 = bf16[512,256]{1,0:T(8,128)(2,1)S(1)} collective-permute-done((bf16[512,256]{1,0:T(8,128)(2,1)S(1)}, bf16[512,256]{1,0:T(8,128)(2,1)S(1)}, u32[]{:S(2)}, u32[]{:S(2)}) %collective-permute-start.1) | collective-permute-done | bytes 262176 | tf_op jit(solution)/shard_map/ppermute | solution.py:23
  20.9 6.7 %collective-permute-done.2 = bf16[512,256]{1,0:T(8,128)(2,1)S(1)} collective-permute-done((bf16[512,256]{1,0:T(8,128)(2,1)S(1)}, bf16[512,256]{1,0:T(8,128)(2,1)S(1)}, u32[]{:S(2)}, u32[]{:S(2)}) %collective-permute-start.2) | collective-permute-done | bytes 262176 | tf_op jit(solution)/shard_map/ppermute | solution.py:23
  27.6 6.7 %collective-permute-done.3 = bf16[512,256]{1,0:T(8,128)(2,1)S(1)} collective-permute-done((bf16[512,256]{1,0:T(8,128)(2,1)S(1)}, bf16[512,256]{1,0:T(8,128)(2,1)S(1)}, u32[]{:S(2)}, u32[]{:S(2)}) %collective-permute-start.3) | collective-permute-done | bytes 262176 | tf_op jit(solution)/shard_map/ppermute | solution.py:23
  34.3 6.7 %collective-permute-done.4 = bf16[512,256]{1,0:T(8,128)(2,1)S(1)} collective-permute-done((bf16[512,256]{1,0:T(8,128)(2,1)S(1)}, bf16[512,256]{1,0:T(8,128)(2,1)S(1)}, u32[]{:S(2)}, u32[]{:S(2)}) %collective-permute-start.4) | collective-permute-done | bytes 262176 | tf_op jit(solution)/shard_map/ppermute | solution.py:23
  41.0 6.7 %collective-permute-done.5 = bf16[512,256]{1,0:T(8,128)(2,1)S(1)} collective-permute-done((bf16[512,256]{1,0:T(8,128)(2,1)S(1)}, bf16[512,256]{1,0:T(8,128)(2,1)S(1)}, u32[]{:S(2)}, u32[]{:S(2)}) %collective-permute-start.5) | collective-permute-done | bytes 262176 | tf_op jit(solution)/shard_map/ppermute | solution.py:23
  47.7 6.7 %collective-permute-done.6 = bf16[512,256]{1,0:T(8,128)(2,1)S(1)} collective-permute-done((bf16[512,256]{1,0:T(8,128)(2,1)S(1)}, bf16[512,256]{1,0:T(8,128)(2,1)S(1)}, u32[]{:S(2)}, u32[]{:S(2)}) %collective-permute-start.6) | collective-permute-done | bytes 262176 | tf_op jit(solution)/shard_map/ppermute | solution.py:23
  54.6 1.0 constant_dynamic-update-slice_fusion.8
  55.8 1.5 constant_dynamic-slice_fusion.1
  57.2 0.1 broadcast_in_dim.13
  57.4 178.0 %while.10 = (s32[]{:T(128)}, f32[16,32768]{1,0:T(8,128)S(1)}, s32[8]{0:T(128)S(1)}, s32[256,2]{0,1:T(2,128)S(1)}, s32[]{:T(128)}, /*index=5*/bf16[256,128,128]{2...) while((s32[]{:T(128)}, f32[16,32768]{1,0:T(8,128)S(1)}, s32[8]{0:T(128)S(1)}, ...), condition=%wide.region_2.3_spmd, body=%wide.region_0.2_spmd.sunk | while | flops 270009600 | bytes 32511596 | solution.py:38
  57.4 0.7 dynamic_slice.26
  60.2 3.6 %gather_fusion = bf16[32,128,256]{2,1,0:T(8,128)(2,1)} fusion(bf16[32,128,256]{2,1,0:T(8,128)(2,1)} %get-tuple-element.132, s32[1024]{0:T(1024)S(1)} %pad_clamp_fusion.2), kind=kCustom, calls=%fused_computation.clone.1 | custom fusion | bytes 4194432 | tf_op jit(solution)/shard_map/while/body/eval_jaxpr/gather | solution.py:10
  63.8 1.3 add_compare_fusion.2
  65.1 2.7 fusion.24
  67.8 4.4 %copy.10 = f32[4,8,128,256]{3,1,2,0:T(8,128)} copy(f32[4,8,128,256]{3,2,1,0:T(8,128)S(1)} %bitcast.21) | data formatting | bytes 8388608 | tf_op jit(solution)/shard_map/while
  72.2 7.4 %scatter_fusion = f32[16,32768]{1,0:T(8,128)S(1)} fusion(f32[16,32768]{1,0:T(8,128)S(1)} %get-tuple-element.117, s32[32]{0:T(128)S(1)} %get-tuple-element.104, f32[32,32768]{1,0:T(8,128)} %bitcast.22), kind=kCustom, calls=%fused_computation.1.clone.1 | custom fusion | flops 1048576 | bytes 12583040 | tf_op jit(solution)/shard_map/while/body/eval_jaxpr/scatter-add | solution.py:14
  79.7 0.7 dynamic_slice.26
  82.4 3.6 %gather_fusion = bf16[32,128,256]{2,1,0:T(8,128)(2,1)} fusion(bf16[32,128,256]{2,1,0:T(8,128)(2,1)} %get-tuple-element.132, s32[1024]{0:T(1024)S(1)} %pad_clamp_fusion.2), kind=kCustom, calls=%fused_computation.clone.1 | custom fusion | bytes 4194432 | tf_op jit(solution)/shard_map/while/body/eval_jaxpr/gather | solution.py:10
  86.0 1.3 add_compare_fusion.2
  87.4 2.7 fusion.24
  90.1 4.4 %copy.10 = f32[4,8,128,256]{3,1,2,0:T(8,128)} copy(f32[4,8,128,256]{3,2,1,0:T(8,128)S(1)} %bitcast.21) | data formatting | bytes 8388608 | tf_op jit(solution)/shard_map/while
  94.5 7.4 %scatter_fusion = f32[16,32768]{1,0:T(8,128)S(1)} fusion(f32[16,32768]{1,0:T(8,128)S(1)} %get-tuple-element.117, s32[32]{0:T(128)S(1)} %get-tuple-element.104, f32[32,32768]{1,0:T(8,128)} %bitcast.22), kind=kCustom, calls=%fused_computation.1.clone.1 | custom fusion | flops 1048576 | bytes 12583040 | tf_op jit(solution)/shard_map/while/body/eval_jaxpr/scatter-add | solution.py:14
  101.9 0.7 dynamic_slice.26
  104.7 3.6 %gather_fusion = bf16[32,128,256]{2,1,0:T(8,128)(2,1)} fusion(bf16[32,128,256]{2,1,0:T(8,128)(2,1)} %get-tuple-element.132, s32[1024]{0:T(1024)S(1)} %pad_clamp_fusion.2), kind=kCustom, calls=%fused_computation.clone.1 | custom fusion | bytes 4194432 | tf_op jit(solution)/shard_map/while/body/eval_jaxpr/gather | solution.py:10
  108.3 1.3 add_compare_fusion.2
  109.6 2.7 fusion.24
  112.3 4.4 %copy.10 = f32[4,8,128,256]{3,1,2,0:T(8,128)} copy(f32[4,8,128,256]{3,2,1,0:T(8,128)S(1)} %bitcast.21) | data formatting | bytes 8388608 | tf_op jit(solution)/shard_map/while
  116.7 7.4 %scatter_fusion = f32[16,32768]{1,0:T(8,128)S(1)} fusion(f32[16,32768]{1,0:T(8,128)S(1)} %get-tuple-element.117, s32[32]{0:T(128)S(1)} %get-tuple-element.104, f32[32,32768]{1,0:T(8,128)} %bitcast.22), kind=kCustom, calls=%fused_computation.1.clone.1 | custom fusion | flops 1048576 | bytes 12583040 | tf_op jit(solution)/shard_map/while/body/eval_jaxpr/scatter-add | solution.py:14
  124.2 0.7 dynamic_slice.26
  127.0 3.6 %gather_fusion = bf16[32,128,256]{2,1,0:T(8,128)(2,1)} fusion(bf16[32,128,256]{2,1,0:T(8,128)(2,1)} %get-tuple-element.132, s32[1024]{0:T(1024)S(1)} %pad_clamp_fusion.2), kind=kCustom, calls=%fused_computation.clone.1 | custom fusion | bytes 4194432 | tf_op jit(solution)/shard_map/while/body/eval_jaxpr/gather | solution.py:10
  130.6 1.3 add_compare_fusion.2
  131.9 2.7 fusion.24
  134.6 4.4 %copy.10 = f32[4,8,128,256]{3,1,2,0:T(8,128)} copy(f32[4,8,128,256]{3,2,1,0:T(8,128)S(1)} %bitcast.21) | data formatting | bytes 8388608 | tf_op jit(solution)/shard_map/while
  139.0 7.4 %scatter_fusion = f32[16,32768]{1,0:T(8,128)S(1)} fusion(f32[16,32768]{1,0:T(8,128)S(1)} %get-tuple-element.117, s32[32]{0:T(128)S(1)} %get-tuple-element.104, f32[32,32768]{1,0:T(8,128)} %bitcast.22), kind=kCustom, calls=%fused_computation.1.clone.1 | custom fusion | flops 1048576 | bytes 12583040 | tf_op jit(solution)/shard_map/while/body/eval_jaxpr/scatter-add | solution.py:14
  146.4 0.7 dynamic_slice.26
  149.2 3.6 %gather_fusion = bf16[32,128,256]{2,1,0:T(8,128)(2,1)} fusion(bf16[32,128,256]{2,1,0:T(8,128)(2,1)} %get-tuple-element.132, s32[1024]{0:T(1024)S(1)} %pad_clamp_fusion.2), kind=kCustom, calls=%fused_computation.clone.1 | custom fusion | bytes 4194432 | tf_op jit(solution)/shard_map/while/body/eval_jaxpr/gather | solution.py:10
  152.8 1.3 add_compare_fusion.2
  154.1 2.7 fusion.24
  156.8 4.4 %copy.10 = f32[4,8,128,256]{3,1,2,0:T(8,128)} copy(f32[4,8,128,256]{3,2,1,0:T(8,128)S(1)} %bitcast.21) | data formatting | bytes 8388608 | tf_op jit(solution)/shard_map/while
  161.2 7.4 %scatter_fusion = f32[16,32768]{1,0:T(8,128)S(1)} fusion(f32[16,32768]{1,0:T(8,128)S(1)} %get-tuple-element.117, s32[32]{0:T(128)S(1)} %get-tuple-element.104, f32[32,32768]{1,0:T(8,128)} %bitcast.22), kind=kCustom, calls=%fused_computation.1.clone.1 | custom fusion | flops 1048576 | bytes 12583040 | tf_op jit(solution)/shard_map/while/body/eval_jaxpr/scatter-add | solution.py:14
  168.7 0.7 dynamic_slice.26
  171.5 3.6 %gather_fusion = bf16[32,128,256]{2,1,0:T(8,128)(2,1)} fusion(bf16[32,128,256]{2,1,0:T(8,128)(2,1)} %get-tuple-element.132, s32[1024]{0:T(1024)S(1)} %pad_clamp_fusion.2), kind=kCustom, calls=%fused_computation.clone.1 | custom fusion | bytes 4194432 | tf_op jit(solution)/shard_map/while/body/eval_jaxpr/gather | solution.py:10
  175.1 1.3 add_compare_fusion.2
  176.4 2.7 fusion.24
  179.1 4.4 %copy.10 = f32[4,8,128,256]{3,1,2,0:T(8,128)} copy(f32[4,8,128,256]{3,2,1,0:T(8,128)S(1)} %bitcast.21) | data formatting | bytes 8388608 | tf_op jit(solution)/shard_map/while
  183.5 7.4 %scatter_fusion = f32[16,32768]{1,0:T(8,128)S(1)} fusion(f32[16,32768]{1,0:T(8,128)S(1)} %get-tuple-element.117, s32[32]{0:T(128)S(1)} %get-tuple-element.104, f32[32,32768]{1,0:T(8,128)} %bitcast.22), kind=kCustom, calls=%fused_computation.1.clone.1 | custom fusion | flops 1048576 | bytes 12583040 | tf_op jit(solution)/shard_map/while/body/eval_jaxpr/scatter-add | solution.py:14
  190.9 0.7 dynamic_slice.26
  193.7 3.6 %gather_fusion = bf16[32,128,256]{2,1,0:T(8,128)(2,1)} fusion(bf16[32,128,256]{2,1,0:T(8,128)(2,1)} %get-tuple-element.132, s32[1024]{0:T(1024)S(1)} %pad_clamp_fusion.2), kind=kCustom, calls=%fused_computation.clone.1 | custom fusion | bytes 4194432 | tf_op jit(solution)/shard_map/while/body/eval_jaxpr/gather | solution.py:10
  197.3 1.3 add_compare_fusion.2
  198.6 2.7 fusion.24
  201.3 4.4 %copy.10 = f32[4,8,128,256]{3,1,2,0:T(8,128)} copy(f32[4,8,128,256]{3,2,1,0:T(8,128)S(1)} %bitcast.21) | data formatting | bytes 8388608 | tf_op jit(solution)/shard_map/while
  205.7 7.4 %scatter_fusion = f32[16,32768]{1,0:T(8,128)S(1)} fusion(f32[16,32768]{1,0:T(8,128)S(1)} %get-tuple-element.117, s32[32]{0:T(128)S(1)} %get-tuple-element.104, f32[32,32768]{1,0:T(8,128)} %bitcast.22), kind=kCustom, calls=%fused_computation.1.clone.1 | custom fusion | flops 1048576 | bytes 12583040 | tf_op jit(solution)/shard_map/while/body/eval_jaxpr/scatter-add | solution.py:14
  213.2 0.7 dynamic_slice.26
  216.0 3.6 %gather_fusion = bf16[32,128,256]{2,1,0:T(8,128)(2,1)} fusion(bf16[32,128,256]{2,1,0:T(8,128)(2,1)} %get-tuple-element.132, s32[1024]{0:T(1024)S(1)} %pad_clamp_fusion.2), kind=kCustom, calls=%fused_computation.clone.1 | custom fusion | bytes 4194432 | tf_op jit(solution)/shard_map/while/body/eval_jaxpr/gather | solution.py:10
  219.6 1.3 add_compare_fusion.2
  220.9 2.7 fusion.24
  223.6 4.4 %copy.10 = f32[4,8,128,256]{3,1,2,0:T(8,128)} copy(f32[4,8,128,256]{3,2,1,0:T(8,128)S(1)} %bitcast.21) | data formatting | bytes 8388608 | tf_op jit(solution)/shard_map/while
  228.0 7.4 %scatter_fusion = f32[16,32768]{1,0:T(8,128)S(1)} fusion(f32[16,32768]{1,0:T(8,128)S(1)} %get-tuple-element.117, s32[32]{0:T(128)S(1)} %get-tuple-element.104, f32[32,32768]{1,0:T(8,128)} %bitcast.22), kind=kCustom, calls=%fused_computation.1.clone.1 | custom fusion | flops 1048576 | bytes 12583040 | tf_op jit(solution)/shard_map/while/body/eval_jaxpr/scatter-add | solution.py:14
  235.5 1.5 reshape.18
  237.0 44.8 %reduce-scatter.2.cloned.1.call-done = f32[512,256]{1,0:T(8,128)} async-done(((f32[2048,256]{1,0:T(8,128)}), f32[512,256]{1,0:T(8,128)}) %reduce-scatter.2.cloned.1.call-update) | async-done | bytes 524304 | tf_op jit(solution)/shard_map/reduce_scatter | solution.py:40
  281.8 1.2 divide_convert_fusion
  283.0 1.0 fusion.10
  (59 shorter events, 1.1 us)
Async XLA Ops:
  6.5 276.5 %copy-start = (bf16[512,256]{1,0:T(8,128)(2,1)S(1)}, bf16[512,256]{1,0:T(8,128)(2,1)}, u32[]{:S(2)}) copy-start(bf16[512,256]{1,0:T(8,128)(2,1)} %param.14) | copy-start | bytes 786436
  6.5 49.2 %copy-start.1 = (bf16[512,256]{1,0:T(8,128)(2,1)S(1)}, bf16[512,256]{1,0:T(8,128)(2,1)}, u32[]{:S(2)}) copy-start(bf16[512,256]{1,0:T(8,128)(2,1)} %param.9) | copy-start | bytes 786436
  6.5 275.3 %reduce-scatter.2.cloned.1.call-start = ((), (), s32[]{:S(2)}) async-start(), calls=%async_computation.1 | async-start | bytes 2621440 | tf_op jit(solution)/shard_map/reduce_scatter | solution.py:40
  6.5 7.7 %collective-permute-start = (bf16[512,256]{1,0:T(8,128)(2,1)}, bf16[512,256]{1,0:T(8,128)(2,1)S(1)}, u32[]{:S(2)}, u32[]{:S(2)}) collective-permute-start(bf16[512,256]{1,0:T(8,128)(2,1)} %param.9), channel_id=1, source_target_pairs={{0,4},{4,8},{8,12},{12,16},{16,20},{20,24},{24,28},{28,0},{1,5},{5... | collective-permute-start | bytes 786440 | tf_op jit(solution)/shard_map/ppermute | solution.py:23
  14.2 6.7 %collective-permute-start.1 = (bf16[512,256]{1,0:T(8,128)(2,1)S(1)}, bf16[512,256]{1,0:T(8,128)(2,1)S(1)}, u32[]{:S(2)}, u32[]{:S(2)}) collective-permute-start(bf16[512,256]{1,0:T(8,128)(2,1)S(1)} %collective-permute-done), channel_id=1, source_target_pairs={{0,4},{4,8},{8,12},{12,16},{16,20},{20,24},{24,28},{28,0},{1,5},{5... | collective-permute-start | bytes 786440 | tf_op jit(solution)/shard_map/ppermute | solution.py:23
  20.9 6.7 %collective-permute-start.2 = (bf16[512,256]{1,0:T(8,128)(2,1)S(1)}, bf16[512,256]{1,0:T(8,128)(2,1)S(1)}, u32[]{:S(2)}, u32[]{:S(2)}) collective-permute-start(bf16[512,256]{1,0:T(8,128)(2,1)S(1)} %collective-permute-done.1), channel_id=1, source_target_pairs={{0,4},{4,8},{8,12},{12,16},{16,20},{20,24},{24,28},{28,0},{1,5},{5... | collective-permute-start | bytes 786440 | tf_op jit(solution)/shard_map/ppermute | solution.py:23
  27.6 6.7 %collective-permute-start.3 = (bf16[512,256]{1,0:T(8,128)(2,1)S(1)}, bf16[512,256]{1,0:T(8,128)(2,1)S(1)}, u32[]{:S(2)}, u32[]{:S(2)}) collective-permute-start(bf16[512,256]{1,0:T(8,128)(2,1)S(1)} %collective-permute-done.2), channel_id=1, source_target_pairs={{0,4},{4,8},{8,12},{12,16},{16,20},{20,24},{24,28},{28,0},{1,5},{5... | collective-permute-start | bytes 786440 | tf_op jit(solution)/shard_map/ppermute | solution.py:23
  34.3 6.7 %collective-permute-start.4 = (bf16[512,256]{1,0:T(8,128)(2,1)S(1)}, bf16[512,256]{1,0:T(8,128)(2,1)S(1)}, u32[]{:S(2)}, u32[]{:S(2)}) collective-permute-start(bf16[512,256]{1,0:T(8,128)(2,1)S(1)} %collective-permute-done.3), channel_id=1, source_target_pairs={{0,4},{4,8},{8,12},{12,16},{16,20},{20,24},{24,28},{28,0},{1,5},{5... | collective-permute-start | bytes 786440 | tf_op jit(solution)/shard_map/ppermute | solution.py:23
  41.0 6.7 %collective-permute-start.5 = (bf16[512,256]{1,0:T(8,128)(2,1)S(1)}, bf16[512,256]{1,0:T(8,128)(2,1)S(1)}, u32[]{:S(2)}, u32[]{:S(2)}) collective-permute-start(bf16[512,256]{1,0:T(8,128)(2,1)S(1)} %collective-permute-done.4), channel_id=1, source_target_pairs={{0,4},{4,8},{8,12},{12,16},{16,20},{20,24},{24,28},{28,0},{1,5},{5... | collective-permute-start | bytes 786440 | tf_op jit(solution)/shard_map/ppermute | solution.py:23
  47.7 6.7 %collective-permute-start.6 = (bf16[512,256]{1,0:T(8,128)(2,1)S(1)}, bf16[512,256]{1,0:T(8,128)(2,1)S(1)}, u32[]{:S(2)}, u32[]{:S(2)}) collective-permute-start(bf16[512,256]{1,0:T(8,128)(2,1)S(1)} %collective-permute-done.5), channel_id=1, source_target_pairs={{0,4},{4,8},{8,12},{12,16},{16,20},{20,24},{24,28},{28,0},{1,5},{5... | collective-permute-start | bytes 786440 | tf_op jit(solution)/shard_map/ppermute | solution.py:23
  55.6 1.7 copy-start.2
  235.4 1.6 copy-start.3
  235.4 47.6 %copy-start.4 = (f32[256]{0:T(256)S(1)}, f32[256]{0:T(256)}, u32[]{:S(2)}) copy-start(f32[256]{0:T(256)} %param.15) | copy-start | bytes 3076
Sparse Core Ops, SparseCore 0:
  237.1 44.6 reduce-scatter.1
